TPU v7x, 256 devices: a whole 4x4x8 slice. The times are simulated.
256 devices in a mesh: dp: 16 (over x_hi, z), tensor: 16 (over y, x_lo, core).
Axes of the slice: x: 4 (x_hi: 2, x_lo: 2; x = x_hi * 2 + x_lo), y: 4, z: 8, core: 2. Of those that a mesh axis runs over, the one named last changes fastest.
Arguments:
- tokens: bfloat16 [32768, 4608], P(('dp', 'tensor')), parts along dimension 0, may hold values from -6 to 6
- pre_gain: float32 [4608], replicated, may hold values from 0.1 to 1.9
- query_weight: bfloat16 [4608, 4096], P(None, 'tensor'), as said below
- key_weight: bfloat16 [4608, 2048], P(None, 'tensor'), as said below
- value_weight: bfloat16 [4608, 2048], P(None, 'tensor'), may hold values from -0.09375 to 0.09375
- out_weight: bfloat16 [4096, 4608], P('tensor'), may hold values from -0.09375 to 0.09375
- post_gain: float32 [4608], replicated, may hold values from 0.1 to 1.9
Outputs:
- layer_out: bfloat16 [32768, 4608], P(('dp', 'tensor')), parts along dimension 0
There are 16 independent parts, one for each index of `dp`. A program takes and returns all parts, laid end to end along the dimension named above; an argument that names none is the same for every part. Nothing has to cross between parts.
Inputs may be any that keep to these rules, and one draw needn't show every extreme that they name: `query_weight`: entries lie within 16 / sqrt(4608) of zero. `key_weight`: entries lie within 16 / sqrt(4608) of zero.
All inputs are finite; a program needn't handle non-finite values.
Results may differ from a plain program's by a relative error of at most 0.015.
Values may be sent and summed in bfloat16 or wider, within the bound.
No kernel may reach another device: no remote copies, remote signals or barrier semaphores. Data moves between devices by JAX's collectives and lax.ppermute only.
A program may use at most 192 MiB of HBM per device.

v0:
```python
import jax
import jax.numpy as jnp
from jax import lax
from jax.sharding import PartitionSpec as P

HEAD_DIM = 128
SEQ_LEN = 128
norm_epsilon = 1e-06
soft_cap = 50.0
query_scale = 1.0 / 12.0
rope_base = 10000.0


def rms_scale(vectors, scale_gain):
    mean_square = jnp.mean(vectors * vectors, axis=-1, keepdims=True)
    return vectors * lax.rsqrt(mean_square + norm_epsilon) * scale_gain


def rotate(vectors, positions):
    half_dim = vectors.shape[-1] // 2
    exponent = jnp.arange(half_dim, dtype=jnp.float32) / half_dim
    angles = positions.astype(jnp.float32)[:, None] * jnp.power(rope_base, -exponent)[None, :]
    cosine = jnp.cos(angles)[:, None, :]
    sine_part = jnp.sin(angles)[:, None, :]
    first_half = vectors[..., :half_dim]
    second_half = vectors[..., half_dim:]
    return jnp.concatenate(
        [
            first_half * cosine - second_half * sine_part,
            second_half * cosine + first_half * sine_part,
        ],
        axis=-1,
    )


def project_block(normed, query_weight, key_weight, value_weight):
    block_rows = normed.shape[0]
    positions = jnp.arange(block_rows, dtype=jnp.int32) % SEQ_LEN
    query = jnp.dot(normed, query_weight, preferred_element_type=jnp.float32)
    keys = jnp.dot(normed, key_weight, preferred_element_type=jnp.float32)
    values = jnp.dot(normed, value_weight, preferred_element_type=jnp.float32)
    query = rotate(query.reshape(block_rows, -1, HEAD_DIM), positions).reshape(block_rows, -1)
    keys = rotate(keys.reshape(block_rows, -1, HEAD_DIM), positions).reshape(block_rows, -1)
    return jnp.concatenate(
        [query.astype(jnp.bfloat16), keys.astype(jnp.bfloat16), values.astype(jnp.bfloat16)], axis=1
    )


def attend(query, keys, values, query_pos, key_pos):
    query_count = query.shape[0]
    key_count = keys.shape[0]
    key_heads = keys.shape[1] // HEAD_DIM
    groups = query.shape[1] // keys.shape[1]
    query_four = query.reshape(query_count, key_heads, groups, HEAD_DIM)
    key_three = keys.reshape(key_count, key_heads, HEAD_DIM)
    value_three = values.reshape(key_count, key_heads, HEAD_DIM)
    raw_scores = jnp.einsum(
        "qhgd,khd->hgqk", query_four, key_three, preferred_element_type=jnp.float32
    )
    capped = soft_cap * jnp.tanh(raw_scores * query_scale / soft_cap)
    allowed = jnp.logical_and(
        key_pos[None, :] <= query_pos[:, None],
        key_pos[None, :] // SEQ_LEN == query_pos[:, None] // SEQ_LEN,
    )
    weights = jnp.where(allowed[None, None], jnp.exp(capped), 0.0)
    probability = (weights / jnp.sum(weights, axis=-1, keepdims=True)).astype(jnp.bfloat16)
    mixed = jnp.einsum(
        "hgqk,khd->qhgd", probability, value_three, preferred_element_type=jnp.float32
    )
    return mixed.astype(jnp.bfloat16).reshape(query_count, -1)


def body(tokens, pre_gain, query_weight, key_weight, value_weight, out_weight, post_gain):
    local_rows = tokens.shape[0]
    query_cols = query_weight.shape[1]
    key_cols = key_weight.shape[1]
    normed = rms_scale(tokens.astype(jnp.float32), pre_gain).astype(jnp.bfloat16)
    stacked = project_block(
        lax.all_gather(normed, "tensor", axis=0, tiled=True), query_weight, key_weight, value_weight
    )
    query = stacked[:, :query_cols]
    keys = stacked[:, query_cols : query_cols + key_cols]
    values = stacked[:, query_cols + key_cols :]
    token_count = stacked.shape[0]
    key_count = min(token_count, lax.axis_size("tensor") * local_rows + SEQ_LEN)
    key_first = jnp.clip(jnp.int32(0) // SEQ_LEN * SEQ_LEN, 0, token_count - key_count)
    query_pos = jnp.arange(lax.axis_size("tensor") * local_rows, dtype=jnp.int32)
    key_pos = key_first + jnp.arange(key_count, dtype=jnp.int32)
    block_out = attend(query, keys, values, query_pos, key_pos)
    mixed = lax.psum_scatter(
        jnp.dot(block_out, out_weight, preferred_element_type=jnp.float32).astype(jnp.bfloat16),
        "tensor",
        scatter_dimension=0,
        tiled=True,
    ).astype(jnp.float32)
    branch = rms_scale(mixed, post_gain)
    return (tokens.astype(jnp.float32) + branch).astype(jnp.bfloat16)


def solution(mesh):
    return jax.shard_map(
        body,
        mesh=mesh,
        in_specs=(
            P(("dp", "tensor"), None),
            P(),
            P(None, "tensor"),
            P(None, "tensor"),
            P(None, "tensor"),
            P("tensor", None),
            P(),
        ),
        out_specs=P(("dp", "tensor"), None),
        check_vma=False,
    )
```

profile of v0, /device:TPU:4, one launch (start us, length us, event | category | flops | bytes accessed | tf_op | source)
XLA Modules:
  0.0 423.9 jit_solution(4512877549720790362)
XLA Ops:
  6.5 0.0 copy-start
  6.5 0.0 all-gather.2.cloned.1.call-start
  6.5 1.7 fusion.9
  8.3 2.6 fusion.11
  10.9 0.0 all-gather.2.cloned.1.call-update
  10.9 0.0 reduce-scatter.2.cloned.1.call-start
  11.0 5.6 %multiply_cosine_fusion = (f32[2048,64]{1,0:T(8,128)}, f32[2048,64]{1,0:T(8,128)}) fusion(f32[64]{0:T(128)S(1)} %negate_power_fusion, f32[2048]{0:T(1024)S(1)} %fusion.36), kind=kLoop, calls=%fused_computation.26 | loop fusion | flops 131072 | bytes 1057024 | tf_op jit(solution)/shard_map/cos | solution.py:23
  16.6 5.4 %fusion.3 = pred[2048,2048]{0,1:T(8,128)(4,1)} fusion(s32[2048]{0:T(1024)S(1)} %add_select_fusion), kind=kLoop, calls=%fused_computation.7 | loop fusion | flops 12582912 | bytes 4202496 | tf_op jit(solution)/shard_map/and | solution.py:61
  22.0 96.0 %all-gather.2.cloned.1.call-done = bf16[2048,4608]{1,0:T(8,128)(2,1)} async-done(((bf16[128,4608]{1,0:T(8,128)(2,1)}), bf16[2048,4608]{1,0:T(8,128)(2,1)}) %all-gather.2.cloned.1.call-update) | async-done | bytes 18874384 | tf_op jit(solution)/shard_map/all_gather | solution.py:79
  118.0 10.4 %convolution_bitcast_fusion = f32[2048,1,128]{0,2,1:T(8,128)S(1)} fusion(bf16[2048,4608]{1,0:T(8,128)(2,1)} %all-gather.2.cloned.1.call-done, bf16[4608,128]{1,0:T(8,128)(2,1)} %param.10), kind=kOutput, calls=%fused_computation.14 | convolution fusion | flops 2415919104 | bytes 21102592 | tf_op jit(solution)/shard_map/dot_general | solution.py:40
  128.4 3.0 fusion.29
  131.4 9.7 %fusion.43 = f32[2048,256]{0,1:T(8,128)S(1)} fusion(bf16[2048,4608]{1,0:T(8,128)(2,1)} %all-gather.2.cloned.1.call-done, bf16[4608,256]{1,0:T(8,128)(2,1)} %param.9), kind=kOutput, calls=%fused_computation.66 | convolution fusion | flops 4831838208 | bytes 23330816 | tf_op jit(solution)/shard_map/dot_general | solution.py:39
  141.1 1.2 fusion.42
  142.3 3.2 copy.16
  145.5 1.9 copy.15
  147.4 0.0 copy-start.2
  147.4 4.8 %subtract_convert_fusion = (bf16[2048,2,64]{2,0,1:T(8,128)(2,1)}, bf16[2048,2,64]{2,0,1:T(8,128)(2,1)}) fusion(f32[2048,2,64]{2,0,1:T(8,128)} %copy.16, f32[2048,2,64]{2,0,1:T(8,128)} %copy.15, f32[2048,64]{1,0:T(8,128)} %get-tuple-element.12, f32[2048,64]{1,0:T(8,128)} %get-tuple-element.11), kind=kLoop, calls=%fused_computation.24 | loop fusion | flops 2097152 | bytes 4194304 | tf_op jit(solution)/shard_map/convert
  152.2 0.0 copy-done.2
  152.2 19.2 %fusion = (f32[2,2048]{1,0:T(2,128)S(1)}, f32[2048,2048,2]{1,0,2:T(8,128)}) fusion(pred[2048,2048]{0,1:T(8,128)(4,1)S(1)} %copy-done.2, bf16[2048,2,64]{2,0,1:T(8,128)(2,1)} %get-tuple-element.6, bf16[2048,2,64]{2,0,1:T(8,128)(2,1)} %get-tuple-element.5, bf16[2048,64]{0,1:T(8,128)(2,1)} %get-tuple-element.10, bf16[2048,64]{0,1:T(8,128)(2,1)} %get-tuple-element.9), kind=kOutput, calls=%fused_computation.2 | convolution fusion | flops 2184179712 | bytes 39337984 | tf_op jit(solution)/shard_map/qhgd,khd->hgqk/dot_general | solution.py:57
  171.4 25.0 %fusion.4 = bf16[128,2,2048]{2,0,1:T(8,128)(2,1)S(1)} fusion(f32[2,2048]{1,0:T(2,128)S(1)} %get-tuple-element.13, f32[2048,2048,2]{1,0,2:T(8,128)} %get-tuple-element.14, pred[2048,2048]{0,1:T(8,128)(4,1)} %fusion.3, bf16[2048,4608]{1,0:T(8,128)(2,1)} %all-gather.2.cloned.1.call-done, bf16[4608,128]{1,0:T(8,128)(2,1)} %param.11), kind=kOutput, calls=%fused_computation.13 | convolution fusion | flops 4606132224 | bytes 58867712 | tf_op jit(solution)/shard_map/hgqk,khd->qhgd/dot_general | solution.py:67
  196.4 0.0 copy-done
  196.4 9.5 %convolution_convert_fusion = bf16[2048,4608]{1,0:T(8,128)(2,1)} fusion(bf16[2048,256]{0,1:T(8,128)(2,1)S(1)} %bitcast.48, bf16[256,4608]{1,0:T(8,128)(2,1)S(1)} %copy-done), kind=kOutput, calls=%fused_computation.3 | convolution fusion | flops 4841275392 | bytes 22282240 | tf_op jit(solution)/shard_map/dot_general | solution.py:91
  205.9 0.0 copy-start.1
  205.9 0.0 reduce-scatter.2.cloned.1.call-update
  205.9 206.8 %reduce-scatter.2.cloned.1.call-done = bf16[128,4608]{1,0:T(8,128)(2,1)} async-done(((bf16[2048,4608]{1,0:T(8,128)(2,1)}), bf16[128,4608]{1,0:T(8,128)(2,1)}) %reduce-scatter.2.cloned.1.call-update) | async-done | bytes 1179664 | tf_op jit(solution)/shard_map/reduce_scatter | solution.py:90
  412.7 1.6 fusion.7
  414.3 0.0 copy-done.1
  414.3 2.8 fusion.12
  (5 shorter events, 0.0 us)
Async XLA Ops:
  6.5 189.9 %copy-start = (bf16[256,4608]{1,0:T(8,128)(2,1)S(1)}, bf16[256,4608]{1,0:T(8,128)(2,1)}, u32[]{:S(2)}) copy-start(bf16[256,4608]{1,0:T(8,128)(2,1)} %param.12) | copy-start | bytes 7077892
  6.5 111.4 %all-gather.2.cloned.1.call-start = ((), (), s32[]{:S(2)}) async-start(), calls=%async_computation.1 | async-start | bytes 20054016 | tf_op jit(solution)/shard_map/all_gather | solution.py:79
  10.9 401.8 %reduce-scatter.2.cloned.1.call-start = ((), (), s32[]{:S(2)}) async-start(), calls=%async_computation.2 | async-start | bytes 20054016 | tf_op jit(solution)/shard_map/reduce_scatter | solution.py:90
  147.4 4.8 %copy-start.2 = (pred[2048,2048]{0,1:T(8,128)(4,1)S(1)}, pred[2048,2048]{0,1:T(8,128)(4,1)}, u32[]{:S(2)}) copy-start(pred[2048,2048]{0,1:T(8,128)(4,1)} %fusion.3) | copy-start | bytes 12582916
  205.9 208.4 %copy-start.1 = (bf16[128,4608]{1,0:T(8,128)(2,1)S(1)}, bf16[128,4608]{1,0:T(8,128)(2,1)}, u32[]{:S(2)}) copy-start(bf16[128,4608]{1,0:T(8,128)(2,1)} %param.7) | copy-start | bytes 3538948
Sparse Core Ops, SparseCore 0:
  11.1 106.8 all-gather.1
  206.1 206.6 reduce-scatter.1
where the time goes:
time: 424 us
  waiting for transfers between devices  303 us (71%)
  matrix products  73.8 us (17%)
  other arithmetic  27.6 us (7%)
  between operations  13.5 us (3%)
  local copies, waits for them, and re-layouts  6.26 us (1%)
    reduce_scatter x1, waiting for transfers between devices, body(): lax.psum_scatter(jnp.dot(block_out, out_weight, preferred_element_type=jn...  207 us
    all_gather x1, waiting for transfers between devices, body(): lax.all_gather(normed, 'tensor', axis=0, tiled=True)  96 us
    dot_general x1, matrix products, attend(): jnp.einsum('hgqk,khd->qhgd', probability, value_three, preferred_element_...  25 us
    dot_general x1, matrix products, attend(): jnp.einsum('qhgd,khd->hgqk', query_four, key_three, preferred_element_typ...  19.2 us
    dot_general x1, matrix products, project_block(): keys = jnp.dot(normed, key_weight, preferred_element_type=jnp.float32)  10.4 us
    dot_general x1, matrix products, project_block(): query = jnp.dot(normed, query_weight, preferred_element_type=jnp.float32)  9.69 us
    dot_general x1, matrix products, body(): jnp.dot(block_out, out_weight, preferred_element_type=jnp.float32)  9.5 us
  transfers between devices with their start and end apart: 2, of which 2 were waited for; matrix products, arithmetic and copies ran while one was open for 3% of the time, Pallas kernels for 0%

commit v1 on v0

--- a/solution.py
+++ b/solution.py
@@ -76,7 +76,12 @@
     key_cols = key_weight.shape[1]
     normed = rms_scale(tokens.astype(jnp.float32), pre_gain).astype(jnp.bfloat16)
     stacked = project_block(
-        lax.all_gather(normed, "tensor", axis=0, tiled=True), query_weight, key_weight, value_weight
+        jnp.concatenate(
+            lax.all_to_all(jnp.stack([normed] * lax.axis_size("tensor")), "tensor", 0, 0), axis=0
+        ),
+        query_weight,
+        key_weight,
+        value_weight,
     )
     query = stacked[:, :query_cols]
     keys = stacked[:, query_cols : query_cols + key_cols]

time: 424 us -> 527 us (1.24)
  waiting for transfers between devices: 303 us -> 402 us
  other arithmetic: 27.6 us -> 20.3 us
  local copies, waits for them, and re-layouts: 6.26 us -> 12.2 us
    all_to_all x0 -> x1, waiting for transfers between devices: none -> 195 us  [body(): lax.all_to_all(jnp.stack([normed] * lax.axis_size('tensor')), 'tensor', 0...]
    all_gather x1 -> x0, waiting for transfers between devices: 96 us -> none  [body(): lax.all_gather(normed, 'tensor', axis=0, tiled=True)]
    another operation x0 -> x1, local copies, waits for them, and re-layouts: none -> 6.67 us  [body(): jnp.stack([normed] * lax.axis_size('tensor'))]
  transfers between devices with their start and end apart: 2 -> 2, of which waited for: 2 -> 2; matrix products, arithmetic and copies ran while one was open for 3% -> 2% of each run, Pallas kernels for 0% -> 0%
where the time goes in v1:
time: 527 us
  waiting for transfers between devices  402 us (76%)
  matrix products  73.4 us (14%)
  other arithmetic  20.3 us (4%)
  between operations  13.5 us (3%)
  local copies, waits for them, and re-layouts  12.2 us (2%)
  starting transfers between devices  5.31 us (1%)
    reduce_scatter x1, waiting for transfers between devices, body(): lax.psum_scatter(jnp.dot(block_out, out_weight, preferred_element_type=jn...  207 us
    all_to_all x1, waiting for transfers between devices, body(): lax.all_to_all(jnp.stack([normed] * lax.axis_size('tensor')), 'tensor', 0...  195 us
    dot_general x1, matrix products, attend(): jnp.einsum('hgqk,khd->qhgd', probability, value_three, preferred_element_...  25 us
    dot_general x1, matrix products, attend(): jnp.einsum('qhgd,khd->hgqk', query_four, key_three, preferred_element_typ...  18.8 us
  transfers between devices with their start and end apart: 2, of which 2 were waited for; matrix products, arithmetic and copies ran while one was open for 2% of the time, Pallas kernels for 0%

profile of v1, /device:TPU:4, one launch (start us, length us, event | category | flops | bytes accessed | tf_op | source)
XLA Modules:
  0.0 526.9 jit_solution(14870005220287142098)
XLA Ops:
  6.5 0.0 copy-start
  6.5 1.7 fusion.9
  8.3 1.6 fusion.11
  9.9 6.7 %stack.2 = bf16[16,128,4608]{2,1,0:T(8,128)(2,1)} broadcast(bf16[128,4608]{1,0:T(8,128)(2,1)S(1)} %fusion.11), dimensions={1,2} | broadcast | bytes 20054016 | tf_op jit(solution)/shard_map/stack | solution.py:80
  16.6 5.3 all-to-all-start
  21.8 0.0 reduce-scatter.2.cloned.1.call-start
  21.9 4.3 copy.16
  26.2 2.8 multiply_cosine_fusion
  29.0 5.4 %fusion.3 = pred[2048,2048]{0,1:T(8,128)(4,1)} fusion(s32[2048]{0:T(1024)S(1)} %add_select_fusion), kind=kLoop, calls=%fused_computation.7 | loop fusion | flops 12582912 | bytes 4202496 | tf_op jit(solution)/shard_map/and | solution.py:61
  34.4 195.1 %all-to-all-done = bf16[16,128,4608]{2,1,0:T(8,128)(2,1)} async-done(((bf16[16,128,4608]{2,1,0:T(8,128)(2,1)}), bf16[16,128,4608]{2,1,0:T(8,128)(2,1)}, u32[]{:S(2)}, u32[]{:S(2)}) %all-to-all-start) | async-done | bytes 18874400 | tf_op jit(solution)/shard_map/all_to_all | solution.py:80
  229.5 10.4 %convolution_bitcast_fusion = f32[2048,1,128]{0,2,1:T(8,128)S(1)} fusion(bf16[2048,4608]{1,0:T(8,128)(2,1)} %bitcast, bf16[4608,128]{1,0:T(8,128)(2,1)} %param.10), kind=kOutput, calls=%fused_computation.14 | convolution fusion | flops 2415919104 | bytes 21102592 | tf_op jit(solution)/shard_map/dot_general | solution.py:40
  239.9 3.0 fusion.29
  242.9 0.0 copy-start.3
  242.9 0.0 copy-start.4
  242.9 9.8 %fusion.42 = f32[2048,2,128]{0,2,1:T(8,128)S(1)} fusion(bf16[2048,4608,1]{1,0,2:T(8,128)(2,1)} %bitcast.6, bf16[2,128,4608]{2,1,0:T(8,128)(2,1)} %bitcast.52), kind=kOutput, calls=%fused_computation.65 | convolution fusion | flops 4831838208 | bytes 23330816 | tf_op jit(solution)/shard_map/dot_general | solution.py:39
  252.7 0.0 copy-start.2
  252.7 0.0 copy-done.3
  252.7 0.0 copy-done.4
  252.7 1.4 subtract_convert_fusion
  254.1 1.2 copy-done.2
  255.3 18.8 %fusion = (f32[2,2048]{1,0:T(2,128)S(1)}, f32[2048,2048,2]{1,0,2:T(8,128)}) fusion(pred[2048,2048]{0,1:T(8,128)(4,1)S(1)} %copy-done.2, bf16[2048,2,64]{0,2,1:T(8,128)(2,1)} %get-tuple-element.6, bf16[2048,2,64]{0,2,1:T(8,128)(2,1)} %get-tuple-element.5, bf16[2048,64]{0,1:T(8,128)(2,1)} %get-tuple-element.8, bf16[2048,64]{0,1:T(8,128)(2,1)} %get-tuple-element.7), kind=kOutput, calls=%fused_computation.2 | convolution fusion | flops 2184179712 | bytes 39337984 | tf_op jit(solution)/shard_map/qhgd,khd->hgqk/dot_general | solution.py:57
  274.1 25.0 %fusion.4 = bf16[128,2,2048]{2,0,1:T(8,128)(2,1)S(1)} fusion(f32[2,2048]{1,0:T(2,128)S(1)} %get-tuple-element.11, f32[2048,2048,2]{1,0,2:T(8,128)} %get-tuple-element.12, pred[2048,2048]{0,1:T(8,128)(4,1)} %fusion.3, bf16[2048,4608]{1,0:T(8,128)(2,1)} %bitcast, bf16[4608,128]{1,0:T(8,128)(2,1)} %param.11), kind=kOutput, calls=%fused_computation.13 | convolution fusion | flops 4606132224 | bytes 58867712 | tf_op jit(solution)/shard_map/hgqk,khd->qhgd/dot_general | solution.py:67
  299.1 0.0 copy-done
  299.1 9.5 %convolution_convert_fusion = bf16[2048,4608]{1,0:T(8,128)(2,1)} fusion(bf16[2048,256]{0,1:T(8,128)(2,1)S(1)} %bitcast.53, bf16[256,4608]{1,0:T(8,128)(2,1)S(1)} %copy-done), kind=kOutput, calls=%fused_computation.3 | convolution fusion | flops 4841275392 | bytes 22282240 | tf_op jit(solution)/shard_map/dot_general | solution.py:96
  308.6 0.0 copy-start.1
  308.6 0.0 reduce-scatter.2.cloned.1.call-update
  308.6 207.1 %reduce-scatter.2.cloned.1.call-done = bf16[128,4608]{1,0:T(8,128)(2,1)} async-done(((bf16[2048,4608]{1,0:T(8,128)(2,1)}), bf16[128,4608]{1,0:T(8,128)(2,1)}) %reduce-scatter.2.cloned.1.call-update) | async-done | bytes 1179664 | tf_op jit(solution)/shard_map/reduce_scatter | solution.py:95
  515.7 1.6 fusion.7
  517.3 0.0 copy-done.1
  517.3 2.8 fusion.12
  (5 shorter events, 0.0 us)
Async XLA Ops:
  6.5 292.5 %copy-start = (bf16[256,4608]{1,0:T(8,128)(2,1)S(1)}, bf16[256,4608]{1,0:T(8,128)(2,1)}, u32[]{:S(2)}) copy-start(bf16[256,4608]{1,0:T(8,128)(2,1)} %param.12) | copy-start | bytes 7077892
  16.6 212.9 %all-to-all-start = ((bf16[16,128,4608]{2,1,0:T(8,128)(2,1)}), bf16[16,128,4608]{2,1,0:T(8,128)(2,1)}, u32[]{:S(2)}, u32[]{:S(2)}) async-start(bf16[16,128,4608]{2,1,0:T(8,128)(2,1)} %stack.2), calls=%async_computation | async-start | bytes 37748736 | tf_op jit(solution)/shard_map/all_to_all | solution.py:80
  21.8 493.8 %reduce-scatter.2.cloned.1.call-start = ((), (), s32[]{:S(2)}) async-start(), calls=%async_computation.2 | async-start | bytes 20054016 | tf_op jit(solution)/shard_map/reduce_scatter | solution.py:95
  242.9 9.8 %copy-start.3 = (f32[2048,64]{0,1:T(8,128)S(1)}, f32[2048,64]{0,1:T(8,128)}, u32[]{:S(2)}) copy-start(f32[2048,64]{0,1:T(8,128)} %get-tuple-element.9) | copy-start | bytes 1572868
  242.9 9.8 %copy-start.4 = (f32[2048,64]{0,1:T(8,128)S(1)}, f32[2048,64]{0,1:T(8,128)}, u32[]{:S(2)}) copy-start(f32[2048,64]{0,1:T(8,128)} %get-tuple-element.10) | copy-start | bytes 1572868
  252.7 2.6 copy-start.2
  308.6 208.7 %copy-start.1 = (bf16[128,4608]{1,0:T(8,128)(2,1)S(1)}, bf16[128,4608]{1,0:T(8,128)(2,1)}, u32[]{:S(2)}) copy-start(bf16[128,4608]{1,0:T(8,128)(2,1)} %param.7) | copy-start | bytes 3538948
Sparse Core Ops, SparseCore 0:
  308.7 206.9 reduce-scatter.1
